TPU v7x, 16 devices: a 4x2x1 block of a 4x4x8 slice. The times are simulated.
16 devices in a mesh: dp: 2 (over y, z), tp: 8 (over x, core).
Axes of the slice: x: 4, y: 2, z: 1, core: 2. Of those that a mesh axis runs over, the one named last changes fastest.
The devices are a block of a 4x4x8 slice.
Arguments:
- tokens: bfloat16 [6, 768, 5120], P('dp'), parts along dimension 0
- positions: int32 [6, 768], P('dp'), parts along dimension 0
- lengths: int32 [6], P('dp'), parts along dimension 0
- norm_attn: bfloat16 [5120], replicated
- norm_mlp: bfloat16 [5120], replicated
- q_gain: bfloat16 [128], replicated
- k_gain: bfloat16 [128], replicated
- w_query: bfloat16 [5120, 8192], P(None, 'tp')
- w_key: bfloat16 [5120, 1024], replicated
- w_value: bfloat16 [5120, 1024], replicated
- w_out: bfloat16 [8192, 5120], P('tp')
- w_gate: bfloat16 [5120, 25600], P(None, 'tp')
- w_up: bfloat16 [5120, 25600], P(None, 'tp')
- w_down: bfloat16 [25600, 5120], P('tp')
Outputs:
- output 1: bfloat16 [6, 768, 5120], P('dp'), parts along dimension 0
- output 2: bfloat16 [6, 768, 8, 128], P('dp', None, 'tp'), parts along dimension 0
- output 3: bfloat16 [6, 768, 8, 128], P('dp', None, 'tp'), parts along dimension 0
There are 2 independent parts. A program takes and returns all parts, laid end to end along the dimension named above; an argument that names none is the same for every part.
All inputs are finite; a program needn't handle non-finite values.
Results may differ from a plain program's by a relative error of at most 0.0149066.
Values are sent between devices in bfloat16 or wider.
A program may use at most 768 MiB of HBM per device.

v0:
```python
import functools
import jax
import jax.numpy as jnp
from jax import lax
from jax.sharding import PartitionSpec as P

EPSILON = 1e-6
ROPE_THETA = 1000000.0


def rms_scale(values, gain_vec):
    mean_sq = jnp.mean(values * values, axis=-1, keepdims=True)
    return values * lax.rsqrt(mean_sq + EPSILON) * gain_vec.astype(jnp.float32)


def rope_tables(positions, half_dim):
    inv_freq = ROPE_THETA ** (-jnp.arange(half_dim, dtype=jnp.float32) / half_dim)
    angles = positions.astype(jnp.float32)[:, :, None] * inv_freq
    return jnp.cos(angles)[:, :, None, :], jnp.sin(angles)[:, :, None, :]


def rope_apply(values, cosine, sine_tab):
    half_dim = values.shape[-1] // 2
    first_half = values[..., :half_dim]
    second_half = values[..., half_dim:]
    return jnp.concatenate([first_half * cosine - second_half * sine_tab, second_half * cosine + first_half * sine_tab], axis=-1)


def local_attention(q_rot, k_rot, v_vals, lengths):
    seq_len, head_dim = k_rot.shape[1], k_rot.shape[2]
    scores = jnp.einsum('bshd,btd->bhst', q_rot, k_rot, preferred_element_type=jnp.float32) * head_dim ** -0.5
    row_idx = jnp.arange(seq_len)[:, None]
    col_idx = jnp.arange(seq_len)[None, :]
    allowed = (col_idx <= row_idx)[None, None] & (col_idx[None, None] < lengths[:, None, None, None])
    attn_probs = jax.nn.softmax(jnp.where(allowed, scores, -1e30), axis=-1).astype(jnp.bfloat16)
    return jnp.einsum('bhst,btd->bshd', attn_probs, v_vals, preferred_element_type=jnp.float32).astype(jnp.bfloat16)


def layer_body(tokens, positions, lengths, norm_attn, norm_mlp, q_gain, k_gain, w_query, w_key, w_value, w_out, w_gate, w_up, w_down, tp_size):
    num_prompts, seq_len, hidden_dim = tokens.shape
    head_dim = q_gain.shape[0]
    local_heads = w_query.shape[1] // head_dim
    kv_heads = w_key.shape[1] // head_dim
    kv_index = lax.axis_index('tp') // (tp_size // kv_heads)
    rows_n = num_prompts * seq_len
    tokens_f32 = tokens.reshape(rows_n, hidden_dim).astype(jnp.float32)
    normed = rms_scale(tokens_f32, norm_attn).astype(jnp.bfloat16)
    w_key_head = lax.dynamic_slice_in_dim(w_key, kv_index * head_dim, head_dim, axis=1)
    w_value_head = lax.dynamic_slice_in_dim(w_value, kv_index * head_dim, head_dim, axis=1)
    q_proj = jnp.dot(normed, w_query, preferred_element_type=jnp.float32).reshape(num_prompts, seq_len, local_heads, head_dim)
    k_proj = jnp.dot(normed, w_key_head, preferred_element_type=jnp.float32).reshape(num_prompts, seq_len, 1, head_dim)
    v_vals = jnp.dot(normed, w_value_head, preferred_element_type=jnp.float32).astype(jnp.bfloat16).reshape(num_prompts, seq_len, head_dim)
    cosine, sine_tab = rope_tables(positions, head_dim // 2)
    q_rot = rope_apply(rms_scale(q_proj, q_gain), cosine, sine_tab).astype(jnp.bfloat16)
    k_rot = rope_apply(rms_scale(k_proj, k_gain), cosine, sine_tab).astype(jnp.bfloat16).reshape(num_prompts, seq_len, head_dim)
    valid_mask = (jnp.arange(seq_len)[None, :] < lengths[:, None])[:, :, None]
    k_cache = jnp.where(valid_mask, k_rot, 0).astype(jnp.bfloat16)[:, :, None, :]
    v_cache = jnp.where(valid_mask, v_vals, 0).astype(jnp.bfloat16)[:, :, None, :]
    attn_rows = local_attention(q_rot, k_rot, v_vals, lengths).reshape(rows_n, local_heads * head_dim)
    attn_part = jnp.dot(attn_rows, w_out, preferred_element_type=jnp.float32).astype(jnp.bfloat16)
    attn_sum = lax.psum(attn_part, 'tp')
    hidden = (tokens_f32 + attn_sum.astype(jnp.float32)).astype(jnp.bfloat16).astype(jnp.float32)
    normed_mlp = rms_scale(hidden, norm_mlp).astype(jnp.bfloat16)
    gate_proj = jnp.dot(normed_mlp, w_gate, preferred_element_type=jnp.float32)
    up_proj = jnp.dot(normed_mlp, w_up, preferred_element_type=jnp.float32)
    gated = (jax.nn.silu(gate_proj) * up_proj).astype(jnp.bfloat16)
    mlp_part = jnp.dot(gated, w_down, preferred_element_type=jnp.float32).astype(jnp.bfloat16)
    mlp_sum = lax.psum(mlp_part, 'tp')
    output = (hidden + mlp_sum.astype(jnp.float32)).astype(jnp.bfloat16).reshape(num_prompts, seq_len, hidden_dim)
    return output, k_cache, v_cache


def solution(mesh):
    body = functools.partial(layer_body, tp_size=mesh.shape['tp'])
    in_specs = (P('dp', None, None), P('dp', None), P('dp'), P(), P(), P(), P(), P(None, 'tp'), P(), P(), P('tp', None), P(None, 'tp'), P(None, 'tp'), P('tp', None))
    out_specs = (P('dp', None, None), P('dp', None, 'tp', None), P('dp', None, 'tp', None))
    return jax.shard_map(body, mesh=mesh, in_specs=in_specs, out_specs=out_specs, check_vma=False)
```

profile of v0, /device:TPU:113, one launch (start us, length us, event | category | flops | bytes accessed | tf_op | source)
XLA Modules:
  0.0 1038.6 jit_solution(12852529047483632256)
XLA Ops:
  7.3 0.2 iota_compare_fusion
  7.5 0.7 convert_element_type.94
  8.1 0.7 convert_element_type.91
  8.8 0.7 iota_compare_fusion.1
  9.5 0.7 convert_element_type.92
  10.2 9.9 fusion.5
  20.2 13.7 %copy.37 = bf16[1024,5120]{1,0:T(8,128)(2,1)} copy(bf16[1024,5120]{0,1:T(8,128)(2,1)} %bitcast.77) | data formatting | bytes 20971520 | tf_op jit(solution)/shard_map/dot_general | solution.py:50
  33.9 33.2 %multiply_reduce_fusion = (f32[3,768,8]{1,2,0:T(8,128)S(1)}, f32[3,768,8,128]{1,3,2,0:T(8,128)}) fusion(bf16[8,128,5120,1]{2,1,0,3:T(8,128)(2,1)} %bitcast.78, bf16[3,768,5120]{2,1,0:T(8,128)(2,1)} %param.14, f32[5120]{0:T(1024)S(1)} %convert_element_type.88, f32[3,768]{1,0:T(4,128)S(1)} %add_rsqrt_fusion.3), kind=kOutput, calls=%fused_computation.35 | convolution fusion | flops 24211077120 | bytes 43619328 | tf_op jit(solution)/shard_map/dot_general | solution.py:50
  67.2 21.8 %fusion.9 = bf16[2304,5120]{1,0:T(8,128)(2,1)} fusion(bf16[3,768,5120]{2,1,0:T(8,128)(2,1)} %param.14, f32[5120]{0:T(1024)S(1)} %convert_element_type.88, f32[2304]{0:T(1024)S(1)} %rsqrt.40), kind=kLoop, calls=%fused_computation.19 | loop fusion | flops 47185920 | bytes 47215616 | tf_op jit(solution)/shard_map/convert_element_type | solution.py:47
  89.0 14.8 %convolution_convert_fusion.2 = bf16[2304,128]{1,0:T(8,128)(2,1)} fusion(bf16[2304,5120]{1,0:T(8,128)(2,1)} %fusion.9, bf16[5120,1024]{1,0:T(8,128)(2,1)} %param.23, s32[]{:T(128)S(6)} %select_n.32), kind=kOutput, calls=%fused_computation.43 | convolution fusion | flops 3020193792 | bytes 25493508 | tf_op jit(solution)/shard_map/dot_general | solution.py:52
  103.9 7.8 multiply_reduce_fusion.1
  111.7 2.1 multiply_cosine_fusion.1
  113.8 0.4 multiply_multiply_fusion.1
  114.2 5.3 fusion.37
  119.5 1.9 broadcast_and_fusion
  121.4 4.8 multiply_multiply_fusion
  126.2 2.7 subtract_convert_fusion
  128.9 28.1 %fusion.50 = (f32[3,8,768]{2,1,0:T(8,128)}, f32[3,8,768,768]{2,3,1,0:T(8,128)}) fusion(pred[3,768,768]{1,2,0:T(8,128)(4,1)} %broadcast_and_fusion, bf16[3,768,8,64]{1,3,2,0:T(8,128)(2,1)} %get-tuple-element.12, bf16[3,768,8,64]{1,3,2,0:T(8,128)(2,1)S(1)} %get-tuple-element.11, bf16[3,768,64]{2,1,0:T(8,128)(2,1)S(1)} %bitcast.81, ...), kind=kOutput, calls=%fused_computation.80 | convolution fusion | flops 3691119360 | bytes 63774720 | tf_op jit(solution)/shard_map/sub | solution.py:35
  157.0 21.5 %convert_bitcast_fusion = bf16[3,768,8,128]{1,3,2,0:T(8,128)(2,1)} fusion(bf16[3,768,128,1]{2,1,3,0:T(8,128)(2,1)} %bitcast.83, f32[3,8,768,768]{2,3,1,0:T(8,128)} %get-tuple-element.24, f32[3,8,768]{2,1,0:T(8,128)} %get-tuple-element.23), kind=kOutput, calls=%fused_computation.40 | convolution fusion | flops 3654549504 | bytes 62005248 | tf_op jit(solution)/shard_map/bhst,btd->bshd/dot_general | solution.py:36
  178.5 7.0 copy.27
  185.5 32.8 %convolution_convert_fusion.1 = bf16[2304,5120]{1,0:T(8,128)(2,1)} fusion(bf16[1024,5120]{1,0:T(8,128)(2,1)} %param.24, bf16[288,8,8,128]{3,2,1,0:T(8,128)(2,1)} %bitcast.79), kind=kOutput, calls=%fused_computation.25 | convolution fusion | flops 24170987520 | bytes 38797312 | tf_op jit(solution)/shard_map/dot_general | solution.py:60
  218.4 0.6 copy-done.9
  219.0 240.8 %all-reduce.3.cloned.1.call-done = bf16[2304,5120]{1,0:T(8,128)(2,1)} async-done(((bf16[2304,5120]{1,0:T(8,128)(2,1)}), bf16[2304,5120]{1,0:T(8,128)(2,1)}) %all-reduce.3.cloned.1.call-update) | async-done | bytes 23592976 | tf_op jit(solution)/shard_map/psum | solution.py:61
  459.8 28.1 %fusion.1 = (f32[2304]{0:T(1024)S(1)}, bf16[2304,5120]{1,0:T(8,128)(2,1)}) fusion(bf16[2304,5120]{1,0:T(8,128)(2,1)} %all-reduce.3.cloned.1.call-done, bf16[3,768,5120]{2,1,0:T(8,128)(2,1)} %param.14), kind=kLoop, calls=%fused_computation.7 | loop fusion | flops 82573056 | bytes 70788096 | tf_op jit(solution)/shard_map/reduce_sum | solution.py:12
  487.9 94.5 %fusion.24 = f32[2304,3200]{1,0:T(8,128)} fusion(bf16[5120,3200]{1,0:T(8,128)(2,1)} %param.25, bf16[2304,5120]{1,0:T(8,128)(2,1)} %get-tuple-element.10, f32[5120]{0:T(1024)S(1)} %convert_element_type.102, f32[2304]{0:T(1024)S(1)} %add_rsqrt_fusion.1), kind=kOutput, calls=%fused_computation.36 | convolution fusion | flops 75544657920 | bytes 85881856 | tf_op jit(solution)/shard_map/dot_general | solution.py:64
  582.3 95.2 %multiply_convert_fusion = bf16[2304,3200]{1,0:T(8,128)(2,1)} fusion(f32[2304,3200]{1,0:T(8,128)} %fusion.24, bf16[5120,3200]{1,0:T(8,128)(2,1)} %param.26, bf16[2304,5120]{1,0:T(8,128)(2,1)} %get-tuple-element.10, f32[5120]{0:T(1024)S(1)} %convert_element_type.102, f32[2304]{0:T(1024)S(1)} %add_rsqrt_fusion.1), kind=kOutput, calls=%fused_computation.23 | convolution fusion | flops 75588894720 | bytes 100627456 | tf_op jit(solution)/shard_map/dot_general | solution.py:65
  677.6 88.5 %convolution_convert_fusion = bf16[2304,5120]{1,0:T(8,128)(2,1)} fusion(bf16[2304,3200]{1,0:T(8,128)(2,1)} %multiply_convert_fusion, bf16[3200,5120]{1,0:T(8,128)(2,1)} %param.27), kind=kOutput, calls=%fused_computation.24 | convolution fusion | flops 75509268480 | bytes 71106560 | tf_op jit(solution)/shard_map/dot_general | solution.py:67
  766.1 1.0 copy-done.2
  767.3 0.2 copy-done.5
  767.4 1.5 select_bitcast_fusion
  768.9 235.8 %all-reduce.5.cloned.1.call-done = bf16[2304,5120]{1,0:T(8,128)(2,1)} async-done(((bf16[2304,5120]{1,0:T(8,128)(2,1)}), bf16[2304,5120]{1,0:T(8,128)(2,1)}) %all-reduce.5.cloned.1.call-update) | async-done | bytes 23592976 | tf_op jit(solution)/shard_map/psum | solution.py:68
  1004.7 26.8 %fusion.4 = bf16[2304,5120]{1,0:T(8,128)(2,1)} fusion(bf16[2304,5120]{1,0:T(8,128)(2,1)} %get-tuple-element.10, bf16[2304,5120]{1,0:T(8,128)(2,1)} %all-reduce.5.cloned.1.call-done), kind=kLoop, calls=%fused_computation.10 | loop fusion | flops 47185920 | bytes 70778880 | tf_op jit(solution)/shard_map/convert_element_type | solution.py:69
  (30 shorter events, 0.6 us)
Async XLA Ops:
  7.2 13.0 %copy-start.8 = (bf16[5120]{0:T(1024)(128)(2,1)S(1)}, bf16[5120]{0:T(1024)(128)(2,1)}, u32[]{:S(2)}) copy-start(bf16[5120]{0:T(1024)(128)(2,1)} %param.17) | copy-start | bytes 30724
  7.2 452.6 %all-reduce.3.cloned.1.call-start = ((), (), s32[]{:S(2)}) async-start(), calls=%async_computation | async-start | bytes 47185920 | tf_op jit(solution)/shard_map/psum | solution.py:61
  9.5 109.9 %copy-start.6 = (pred[3,768]{1,0:T(4,128)(4,1)}, pred[3,768]{1,0:T(4,128)(4,1)S(1)}, u32[]{:S(2)}) copy-start(pred[3,768]{1,0:T(4,128)(4,1)S(1)} %iota_compare_fusion.1) | copy-start | bytes 6916
  89.0 14.9 %copy-start = (bf16[2304,5120]{1,0:T(8,128)(2,1)S(1)}, bf16[2304,5120]{1,0:T(8,128)(2,1)}, u32[]{:S(2)}) copy-start(bf16[2304,5120]{1,0:T(8,128)(2,1)} %fusion.9) | copy-start | bytes 70778880
  119.5 37.6 %copy-start.1 = (bf16[3,768,1,64]{3,1,0,2:T(8,128)(2,1)}, bf16[3,768,1,64]{3,1,0,2:T(8,128)(2,1)S(1)}, u32[]{:S(2)}) copy-start(bf16[3,768,1,64]{3,1,0,2:T(8,128)(2,1)S(1)} %get-tuple-element.13) | copy-start | bytes 884740
  119.5 37.6 %copy-start.3 = (bf16[3,768,1,64]{3,1,0,2:T(8,128)(2,1)}, bf16[3,768,1,64]{3,1,0,2:T(8,128)(2,1)S(1)}, u32[]{:S(2)}) copy-start(bf16[3,768,1,64]{3,1,0,2:T(8,128)(2,1)S(1)} %get-tuple-element.14) | copy-start | bytes 884740
  218.3 0.7 copy-start.9
  218.4 786.4 %all-reduce.5.cloned.1.call-start = ((), (), s32[]{:S(2)}) async-start(), calls=%async_computation.1 | async-start | bytes 47185920 | tf_op jit(solution)/shard_map/psum | solution.py:68
  766.0 1.1 copy-start.2
  766.0 1.2 copy-start.4
  766.0 1.4 copy-start.5
  766.0 1.4 copy-start.7
Sparse Core Ops, SparseCore 0:
  218.5 241.2 all-reduce.2
  766.2 238.4 all-reduce.4
where the time goes:
time: 1050 us; the launch traced here: 1040 us
  waiting for transfers between devices  477 us (45%)
  matrix products  416 us (40%)
  other arithmetic  108 us (10%)
  local copies, waits for them, and re-layouts  22.7 us (2%)
  between operations  14.4 us (1%)
    psum x1, waiting for transfers between devices, layer_body(): attn_sum = lax.psum(attn_part, 'tp')  241 us
    psum x1, waiting for transfers between devices, layer_body(): mlp_sum = lax.psum(mlp_part, 'tp')  236 us
    dot_general x1, matrix products, layer_body(): up_proj = jnp.dot(normed_mlp, w_up, preferred_element_type=jnp.float32)  95.2 us
    dot_general x1, matrix products, layer_body(): gate_proj = jnp.dot(normed_mlp, w_gate, preferred_element_type=jnp.float32)  94.5 us
    dot_general x1, matrix products, layer_body(): jnp.dot(gated, w_down, preferred_element_type=jnp.float32)  88.5 us
    reduce_sum x2, other arithmetic, rms_scale(): mean_sq = jnp.mean(values * values, axis=-1, keepdims=True)  38 us
    dot_general x1, matrix products, layer_body(): jnp.dot(normed, w_query, preferred_element_type=jnp.float32)  33.2 us
    dot_general x1, matrix products, layer_body(): jnp.dot(attn_rows, w_out, preferred_element_type=jnp.float32)  32.8 us
  transfers between devices with their start and end apart: 2, of which 2 were waited for; matrix products, arithmetic and copies ran while one was open for 0% of the time, Pallas kernels for 0%

commit v1 on v0

v1 whole, which is shorter than its diff:
```python
import functools
import jax
import jax.numpy as jnp
from jax import lax
from jax.experimental import pallas as pl
from jax.experimental.pallas import tpu as pltpu
from jax.sharding import PartitionSpec as P

EPSILON = 1e-6
ROPE_THETA = 1000000.0
MESH = pl.DeviceIdType.MESH
CORES = 2
TILE = 256
UNITS = 2
GU_BUFS = 3
WD_BUFS = 4
BF = jnp.bfloat16
F32 = jnp.float32


def rope_tables(positions, half_dim):
    inv_freq = ROPE_THETA ** (-jnp.arange(half_dim, dtype=F32) / half_dim)
    angles = positions.astype(F32)[:, None] * inv_freq
    cosine, sine = jnp.cos(angles), jnp.sin(angles)
    return jnp.concatenate([cosine, cosine], axis=-1), jnp.concatenate([-sine, sine], axis=-1)


def dot(a, b):
    return jnp.dot(a, b, preferred_element_type=F32)


def layer_kernel(tp, prompts, seq, head_dim, kv_heads, dims,
                 tokens, cos_h, sin_h, lens, n_attn, n_mlp, q_gain, k_gain, wq, wk, wv, wo, wg, wu, wdn,
                 ho, kc, vc,
                 n2, act, kk, vv, kco, vco, cosb, sinb, gu, wd, pp, xp, land, ownh,
                 s_x, s_cs, s_gu, s_wd, s_stage, s_xp, s_res, s_kv, s_own,
                 rs_send, rs_recv, ag_send, ag_recv, dd_send, dd_recv):
    hidden, width_q, width_f = dims
    chips = tp // CORES
    half = hidden // CORES
    unit = half // UNITS
    unit_tiles = unit // TILE
    rows_b = seq // chips
    heads = width_q // head_dim
    q_tiles = width_q // TILE
    f_tiles = width_f // head_dim
    n_tiles = hidden // TILE
    per_ar = 6 * UNITS
    lanes = head_dim

    me = lax.axis_index('tp')
    core = lax.rem(me, CORES)
    chip = me // CORES
    ring = lax.rem(chip + core * (chips - 2 * chip), chips)
    nxt = CORES * lax.rem(chip + chips + 1 - 2 * core, chips) + core
    prv = CORES * lax.rem(chip + chips - 1 + 2 * core, chips) + core
    partner = me + 1 - 2 * core
    kv_col = pl.multiple_of((me // (tp // kv_heads)) * head_dim, head_dim)

    barrier = pltpu.get_barrier_semaphore()
    for other in (nxt, prv, partner):
        pl.semaphore_signal(barrier, inc=1, device_id={'tp': other}, device_id_type=MESH)
    pl.semaphore_wait(barrier, 3)

    def remote(src, dst, send, recv, to):
        return pltpu.make_async_remote_copy(src_ref=src, dst_ref=dst, send_sem=send, recv_sem=recv,
                                            device_id={'tp': to}, device_id_type=MESH)

    def local(src, dst, sem):
        return pltpu.make_async_copy(src, dst, sem)

    def block_rows(b):
        return pl.ds(pl.multiple_of(b * rows_b, rows_b), rows_b)

    def ho_block(c, g, b, side):
        rows = pl.ds(pl.multiple_of(c * seq + b * rows_b, rows_b), rows_b)
        return ho.at[rows, pl.ds(pl.multiple_of(side * half + g * unit, TILE), unit)]

    def send_partial(e, c, g):
        i, par = lax.rem(c, prompts), lax.rem(c, 2)
        rows = block_rows(lax.rem(ring + 2 * chips - 1 - e, chips))
        u = i * UNITS + g
        if e == 0:
            local(xp.at[u], xp.at[u], s_xp.at[u]).wait()
        else:
            local(land.at[par, g, e - 1], land.at[par, g, e - 1], rs_recv.at[par, g, e - 1]).wait()
        mine, theirs, came = pp.at[u, rows], xp.at[u, rows], land.at[par, g, max(e - 1, 0)]

        def add(r, _):
            rr = pl.ds(pl.multiple_of(r * 16, 16), 16)
            total = mine[rr, :].astype(F32) + theirs[rr, :].astype(F32)
            if e > 0:
                total = total + came[rr, :].astype(F32)
            mine[rr, :] = total.astype(BF)
            return 0
        lax.fori_loop(0, rows_b // 16, add, 0)
        remote(mine, land.at[par, g, e], rs_send.at[par, g, e], rs_recv.at[par, g, e], nxt).start()

    def finish_sum(c, g):
        i, par = lax.rem(c, prompts), lax.rem(c, 2)
        u = i * UNITS + g
        rows = block_rows(ring)
        local(land.at[par, g, 2], land.at[par, g, 2], rs_recv.at[par, g, 2]).wait()

        @pl.when(c < prompts)
        def _():
            local(ownh.at[u], ownh.at[u], s_res.at[u]).wait()
        mine, theirs, came, own = pp.at[u, rows], xp.at[u, rows], land.at[par, g, 2], ownh.at[u]

        def add(r, _):
            rr = pl.ds(pl.multiple_of(r * 16, 16), 16)
            total = came[rr, :].astype(F32) + (mine[rr, :].astype(F32) + theirs[rr, :].astype(F32))
            own[rr, :] = (own[rr, :].astype(F32) + total).astype(BF)
            return 0
        lax.fori_loop(0, rows_b // 16, add, 0)
        place = ho_block(c, g, ring, core)
        remote(own, place, ag_send.at[par, g, 0], ag_recv.at[par, g, 0], nxt).start()
        remote(own, place, dd_send.at[par, g, 0], dd_recv.at[par, g, 0], partner).start()
        local(own, place, s_own.at[par, g]).start()

    def pass_on(e, c, g):
        par = lax.rem(c, 2)
        place = ho_block(c, g, lax.rem(ring + 2 * chips - e, chips), core)
        local(place, place, ag_recv.at[par, g, e - 1]).wait()
        if e < 3:
            remote(place, place, ag_send.at[par, g, e], ag_recv.at[par, g, e], nxt).start()
        remote(place, place, dd_send.at[par, g, e], dd_recv.at[par, g, e], partner).start()

    def settle(c, g):
        par = lax.rem(c, 2)
        u = lax.rem(c, prompts) * UNITS + g
        place = ho_block(c, g, ring, core)
        local(ownh.at[u], ownh.at[u], s_own.at[par, g]).wait()
        for e in range(3):
            local(land.at[par, g, e], land.at[par, g, e], rs_send.at[par, g, e]).wait()
            local(place, place, ag_send.at[par, g, e]).wait()
        for e in range(4):
            local(place, place, dd_send.at[par, g, e]).wait()
        for e in range(4):
            local(place, place, dd_recv.at[par, g, e]).wait()

    def slot(k):
        c, j = k // per_ar, lax.rem(k, per_ar)
        e, g = j // UNITS, lax.rem(j, UNITS)
        live = c < 2 * prompts
        for s in range(3):
            @pl.when(live & (e == s))
            def _(s=s):
                send_partial(s, c, g)

        @pl.when(live & (e == 3))
        def _():
            finish_sum(c, g)
        for s in range(2):
            @pl.when(live & (e == 4 + s))
            def _(s=s):
                pass_on(s + 1, c, g)

        @pl.when((e == 0) & (c > 0))
        def _():
            pass_on(3, c - 1, g)

        @pl.when((e == 1) & (c > 0))
        def _():
            settle(c - 1, g)

    def run_slots(lo, hi):
        def body(k, _):
            slot(k)
            return 0
        lax.fori_loop(lo, hi, body, 0)

    def q_tile(t):
        b = lax.rem(t, GU_BUFS)
        return local(wq.at[:, pl.ds(pl.multiple_of(t * TILE, TILE), TILE)], gu.at[b], s_gu.at[b, 0])

    def kv_tile():
        b = q_tiles % GU_BUFS
        return (local(wk.at[:, pl.ds(kv_col, lanes)], gu.at[b, :, pl.ds(0, lanes)], s_gu.at[b, 0]),
                local(wv.at[:, pl.ds(kv_col, lanes)], gu.at[b, :, pl.ds(lanes, lanes)], s_gu.at[b, 1]))

    def f_tile(t):
        b = lax.rem(t, GU_BUFS)
        cols = pl.ds(pl.multiple_of(t * lanes, lanes), lanes)
        return (local(wg.at[:, cols], gu.at[b, :, pl.ds(0, lanes)], s_gu.at[b, 0]),
                local(wu.at[:, cols], gu.at[b, :, pl.ds(lanes, lanes)], s_gu.at[b, 1]))

    def tile_place(n):
        g, w = n // (2 * unit_tiles), lax.rem(n, 2 * unit_tiles)
        away = w < unit_tiles
        t = lax.rem(w, unit_tiles)
        side = jnp.where(away, 1 - core, core)
        return g, away, t, pl.ds(pl.multiple_of(side * half + g * unit + t * TILE, TILE), TILE)

    def o_tile(n):
        b = lax.rem(n, WD_BUFS)
        return local(wo.at[:, tile_place(n)[3]], wd.at[b, pl.ds(0, width_q), :], s_wd.at[b])

    def d_tile(n):
        b = lax.rem(n, WD_BUFS)
        return local(wdn.at[:, tile_place(n)[3]], wd.at[b], s_wd.at[b])

    def project(lhs, depth, fetch, i, group0, bounds):
        def body(n, _):
            @pl.when(n + WD_BUFS - 1 < n_tiles)
            def _():
                fetch(n + WD_BUFS - 1).start()
            fetch(n).wait()
            g, away, t, _cols = tile_place(n)
            u = jnp.where(away, prompts * UNITS, i * UNITS + g)
            cols = pl.ds(pl.multiple_of(t * TILE, TILE), TILE)

            @pl.when(away & (group0 + g > 0))
            def _():
                local(pp.at[u, :, cols], pp.at[u, :, cols], s_stage.at[t]).wait()
            pp[u, :, cols] = dot(lhs[...], wd[lax.rem(n, WD_BUFS), :depth, :]).astype(BF)

            @pl.when(away)
            def _():
                to = i * UNITS + g
                remote(pp.at[u, :, cols], xp.at[to, :, cols], s_stage.at[t], s_xp.at[to], partner).start()
            run_slots(*bounds(n))
            return 0
        lax.fori_loop(0, n_tiles, body, 0)

    def rms_rows(gain):
        def body(r, _):
            rr = pl.ds(pl.multiple_of(r * 16, 16), 16)
            v = n2[rr, :].astype(F32)
            scale = lax.rsqrt(jnp.mean(v * v, axis=-1, keepdims=True) + EPSILON)
            n2[rr, :] = (v * scale * gain[...].astype(F32)).astype(BF)
            return 0
        lax.fori_loop(0, seq // 16, body, 0)

    def turned(v, gain):
        v = v * lax.rsqrt(jnp.mean(v * v, axis=-1, keepdims=True) + EPSILON) * gain[...].astype(F32)
        return v * cosb[...] + pltpu.roll(v, lanes // 2, 1) * sinb[...]

    def load_x(i):
        rows = pl.ds(pl.multiple_of(i * seq, seq), seq)
        return (local(tokens.at[rows, :], n2, s_x),
                local(cos_h.at[rows, :], cosb, s_cs.at[0]),
                local(sin_h.at[rows, :], sinb, s_cs.at[1]))

    def load_h(i):
        return local(ho.at[pl.ds(pl.multiple_of(i * seq, seq), seq), :], n2, s_x)

    for cp in load_x(0):
        cp.start()
    for t in range(GU_BUFS - 1):
        q_tile(t).start()
    for n in range(WD_BUFS - 1):
        o_tile(n).start()
    for i in range(prompts):
        for g in range(UNITS):
            rows = pl.ds(pl.multiple_of(i * seq + ring * rows_b, rows_b), rows_b)
            cols = pl.ds(pl.multiple_of(core * half + g * unit, TILE), unit)
            local(tokens.at[rows, cols], ownh.at[i * UNITS + g], s_res.at[i * UNITS + g]).start()

    w_q, w_h, w_o = 4, 2, 1
    weight_a = w_q * (q_tiles + 1) + w_h * heads + w_o * n_tiles

    def attention_phase(i, _):
        def upto(w):
            return jnp.maximum(0, ((i - 1) * weight_a + w) * per_ar // ((prompts - 1) * weight_a))

        for cp in load_x(i):
            cp.wait()
        rms_rows(n_attn)
        length = lens[i]

        def q_body(t, _):
            @pl.when(t + GU_BUFS - 1 < q_tiles)
            def _():
                q_tile(t + GU_BUFS - 1).start()

            @pl.when(t + GU_BUFS - 1 == q_tiles)
            def _():
                for cp in kv_tile():
                    cp.start()
            q_tile(t).wait()
            y = dot(n2[...], gu[lax.rem(t, GU_BUFS)])
            for s in range(TILE // lanes):
                act[:, pl.ds(pl.multiple_of(t * TILE + s * lanes, lanes), lanes)] = turned(y[:, s * lanes:(s + 1) * lanes], q_gain).astype(BF)
            run_slots(upto(t * w_q), upto((t + 1) * w_q))
            return 0
        lax.fori_loop(0, q_tiles, q_body, 0)
        for cp in kv_tile():
            cp.wait()
        y = dot(n2[...], gu[q_tiles % GU_BUFS])
        k_rot = turned(y[:, :lanes], k_gain).astype(BF)
        v_val = y[:, lanes:].astype(BF)
        kk[...] = k_rot
        vv[...] = v_val
        valid = lax.broadcasted_iota(jnp.int32, (seq, lanes), 0) < length
        kco[...] = jnp.where(valid, k_rot.astype(F32), 0.0).astype(BF)
        vco[...] = jnp.where(valid, v_val.astype(F32), 0.0).astype(BF)
        rows = pl.ds(pl.multiple_of(i * seq, seq), seq)
        caches = (local(kco, kc.at[rows, :], s_kv.at[0]), local(vco, vc.at[rows, :], s_kv.at[1]))
        for cp in caches:
            cp.start()

        @pl.when(i + 1 < prompts)
        def _():
            for cp in load_x(i + 1):
                cp.start()
            for t in range(GU_BUFS - 1):
                q_tile(t).start()

        @pl.when(i + 1 == prompts)
        def _():
            for t in range(GU_BUFS - 1):
                for cp in f_tile(t):
                    cp.start()
        run_slots(upto(q_tiles * w_q), upto((q_tiles + 1) * w_q))
        base = (q_tiles + 1) * w_q
        q_rows = seq // 3

        def head_body(hd, _):
            q_cols = pl.ds(pl.multiple_of(hd * lanes, lanes), lanes)
            o_cols = pl.ds(pl.multiple_of(width_q + hd * lanes, lanes), lanes)
            for qb in range(3):
                span = (qb + 1) * q_rows
                q = act[qb * q_rows:span, q_cols]
                s = lax.dot_general(q, kk[:span, :], (((1,), (1,)), ((), ())), preferred_element_type=F32) * head_dim ** -0.5
                row = lax.broadcasted_iota(jnp.int32, (q_rows, span), 0) + qb * q_rows
                col = lax.broadcasted_iota(jnp.int32, (q_rows, span), 1)
                s = jnp.where((col <= row) & (col < length), s, -1e30)
                p = jnp.exp(s - jnp.max(s, axis=-1, keepdims=True))
                p = p * (1.0 / jnp.sum(p, axis=-1, keepdims=True))
                act[qb * q_rows:span, o_cols] = dot(p.astype(BF), vv[:span, :]).astype(BF)
            run_slots(upto(base + hd * w_h), upto(base + (hd + 1) * w_h))
            return 0
        lax.fori_loop(0, heads, head_body, 0)
        for cp in caches:
            cp.wait()
        base2 = base + heads * w_h
        project(act.at[:, pl.ds(width_q, width_q)], width_q, o_tile, i, i * UNITS,
                lambda n: (upto(base2 + n * w_o), upto(base2 + (n + 1) * w_o)))

        @pl.when(i + 1 < prompts)
        def _():
            for n in range(WD_BUFS - 1):
                o_tile(n).start()

        @pl.when(i + 1 == prompts)
        def _():
            for n in range(WD_BUFS - 1):
                d_tile(n).start()
        return 0
    lax.fori_loop(0, prompts, attention_phase, 0)

    lead = 2 * UNITS
    run_slots(per_ar, per_ar + lead)
    load_h(0).start()
    stride = (2 * prompts - 2 - 1) * per_ar - lead

    def mlp_phase(i, _):
        k0 = per_ar + lead + i * stride // (prompts - 1)
        k1 = (i + 2) * per_ar + lead
        k2 = jnp.minimum(per_ar + lead + (i + 1) * stride // (prompts - 1), (2 * prompts - 1) * per_ar)
        k1 = jnp.minimum(k1, k2)
        load_h(i).wait()
        rms_rows(n_mlp)

        def f_body(t, _):
            @pl.when(t + GU_BUFS - 1 < f_tiles)
            def _():
                for cp in f_tile(t + GU_BUFS - 1):
                    cp.start()
            for cp in f_tile(t):
                cp.wait()
            y = dot(n2[...], gu[lax.rem(t, GU_BUFS)])
            gate, up = y[:, :lanes], y[:, lanes:]
            act[:, pl.ds(pl.multiple_of(t * lanes, lanes), lanes)] = (gate * jax.nn.sigmoid(gate) * up).astype(BF)
            run_slots(k0 + t * (k1 - k0) // f_tiles, k0 + (t + 1) * (k1 - k0) // f_tiles)
            return 0
        lax.fori_loop(0, f_tiles, f_body, 0)

        @pl.when(i + 1 < prompts)
        def _():
            load_h(i + 1).start()
            for t in range(GU_BUFS - 1):
                for cp in f_tile(t):
                    cp.start()
        project(act, width_f, d_tile, i, (prompts + i) * UNITS,
                lambda n: (k1 + n * (k2 - k1) // n_tiles, k1 + (n + 1) * (k2 - k1) // n_tiles))

        @pl.when(i + 1 < prompts)
        def _():
            for n in range(WD_BUFS - 1):
                d_tile(n).start()
        return 0
    lax.fori_loop(0, prompts, mlp_phase, 0)

    run_slots((2 * prompts - 1) * per_ar, 2 * prompts * per_ar + lead)
    for t in range(unit_tiles):
        cols = pl.ds(t * TILE, TILE)
        local(pp.at[prompts * UNITS, :, cols], pp.at[prompts * UNITS, :, cols], s_stage.at[t]).wait()


def layer_body(tokens, positions, lengths, norm_attn, norm_mlp, q_gain, k_gain, w_query, w_key, w_value, w_out, w_gate, w_up, w_down, tp_size):
    prompts, seq, hidden = tokens.shape
    head_dim = q_gain.shape[0]
    width_q, width_f = w_query.shape[1], w_gate.shape[1]
    kv_heads = w_key.shape[1] // head_dim
    chips = tp_size // CORES
    half = hidden // CORES
    unit = half // UNITS
    rows_n = prompts * seq
    cos_t, sin_t = rope_tables(positions.reshape(rows_n), head_dim // 2)
    any_spec = pl.BlockSpec(memory_space=pl.ANY)
    vmem = pl.BlockSpec(memory_space=pltpu.VMEM)
    smem = pl.BlockSpec(memory_space=pltpu.SMEM)
    kernel = functools.partial(layer_kernel, tp_size, prompts, seq, head_dim, kv_heads, (hidden, width_q, width_f))
    dma = pltpu.SemaphoreType.DMA
    pieces = prompts * UNITS
    ho, kc, vc = pl.pallas_call(
        kernel,
        name='decoder_layer',
        out_shape=(jax.ShapeDtypeStruct((2 * rows_n, hidden), BF),
                   jax.ShapeDtypeStruct((rows_n, head_dim), BF),
                   jax.ShapeDtypeStruct((rows_n, head_dim), BF)),
        in_specs=[any_spec, any_spec, any_spec, smem, vmem, vmem, vmem, vmem] + [any_spec] * 7,
        out_specs=(any_spec, any_spec, any_spec),
        scratch_shapes=[
            pltpu.VMEM((seq, hidden), BF),
            pltpu.VMEM((seq, width_f), BF),
            pltpu.VMEM((seq, head_dim), BF), pltpu.VMEM((seq, head_dim), BF),
            pltpu.VMEM((seq, head_dim), BF), pltpu.VMEM((seq, head_dim), BF),
            pltpu.VMEM((seq, head_dim), F32), pltpu.VMEM((seq, head_dim), F32),
            pltpu.VMEM((GU_BUFS, hidden, TILE), BF),
            pltpu.VMEM((WD_BUFS, width_f, TILE), BF),
            pltpu.VMEM((pieces + 1, seq, unit), BF),
            pltpu.VMEM((pieces, seq, unit), BF),
            pltpu.VMEM((2, UNITS, 3, seq // chips, unit), BF),
            pltpu.VMEM((pieces, seq // chips, unit), BF),
            dma, dma((2,)), dma((GU_BUFS, 2)), dma((WD_BUFS,)), dma((unit // TILE,)), dma((pieces,)), dma((pieces,)), dma((2,)), dma((2, UNITS)),
            dma((2, UNITS, 3)), dma((2, UNITS, 3)), dma((2, UNITS, 3)), dma((2, UNITS, 3)), dma((2, UNITS, 4)), dma((2, UNITS, 4)),
        ],
        compiler_params=pltpu.CompilerParams(collective_id=0, has_side_effects=True, vmem_limit_bytes=67043328),
    )(tokens.reshape(rows_n, hidden), cos_t, sin_t, lengths, norm_attn[None], norm_mlp[None], q_gain[None], k_gain[None],
      w_query, w_key, w_value, w_out, w_gate, w_up, w_down)
    shape = (prompts, seq, 1, head_dim)
    return ho[rows_n:].reshape(prompts, seq, hidden), kc.reshape(shape), vc.reshape(shape)


def solution(mesh):
    body = functools.partial(layer_body, tp_size=mesh.shape['tp'])
    in_specs = (P('dp', None, None), P('dp', None), P('dp'), P(), P(), P(), P(), P(None, 'tp'), P(), P(), P('tp', None), P(None, 'tp'), P(None, 'tp'), P('tp', None))
    out_specs = (P('dp', None, None), P('dp', None, 'tp', None), P('dp', None, 'tp', None))
    return jax.shard_map(body, mesh=mesh, in_specs=in_specs, out_specs=out_specs, check_vma=False)
```

time: 1050 us -> 618 us (0.59); the launches traced: 1040 us -> 617 us
  Pallas kernels: 0 us -> 585 us
  waiting for transfers between devices: 477 us -> 0 us
  matrix products: 416 us -> 0 us
  other arithmetic: 108 us -> 7.01 us
  between operations: 14.4 us -> 0.66 us
    pallas_call x0 -> x1, Pallas kernels: none -> 585 us  [layer_body(): pl.pallas_call(kernel, name='decoder_layer', out_shape=(jax.ShapeDtypeStr...]
    psum x2 -> x0, waiting for transfers between devices: 477 us -> none  [the longest x1 241 us: layer_body(): attn_sum = lax.psum(attn_part, 'tp')]
    dot_general x8 -> x0, matrix products: 388 us -> none  [the longest x1 95.2 us: layer_body(): up_proj = jnp.dot(normed_mlp, w_up, preferred_element_type=jnp.float32)]
    convert_element_type x7 -> x1, other arithmetic: 50.6 us -> 0.71 us  [rope_tables(): angles = positions.astype(F32)[:, None] * inv_freq]
    reduce_sum x2 -> x0, other arithmetic: 38 us -> none  [rms_scale(): mean_sq = jnp.mean(values * values, axis=-1, keepdims=True)]
    sub x1 -> x0, matrix products: 28.1 us -> none  [local_attention(): jax.nn.softmax(jnp.where(allowed, scores, -1e+30), axis=-1)]
    slice x0 -> x1, local copies, waits for them, and re-layouts: none -> 19.6 us  [layer_body(): ho[rows_n:].reshape(prompts, seq, hidden)]
    dot_general x1 -> x0, local copies, waits for them, and re-layouts: 13.7 us -> none  [layer_body(): jnp.dot(normed, w_query, preferred_element_type=jnp.float32)]
  transfers between devices with their start and end apart: 2 -> 0, of which waited for: 2 -> 0; matrix products, arithmetic and copies ran while one was open for 0% -> 0% of each run, Pallas kernels for 0% -> 0%
where the time goes in v1:
time: 618 us; the launch traced here: 617 us
  Pallas kernels  585 us (95%)
  local copies, waits for them, and re-layouts  24.4 us (4%)
  other arithmetic  7.01 us (1%)
    pallas_call x1, Pallas kernels, layer_body(): pl.pallas_call(kernel, name='decoder_layer', out_shape=(jax.ShapeDtypeStr...  585 us
    slice x1, local copies, waits for them, and re-layouts, layer_body(): ho[rows_n:].reshape(prompts, seq, hidden)  19.6 us

profile of v1, /device:TPU:113, one launch (start us, length us, event | category | flops | bytes accessed | tf_op | source)
XLA Modules:
  0.0 617.2 jit_solution(5667961040498287761)
XLA Ops:
  0.6 0.7 convert_element_type.10
  1.4 1.3 broadcast_in_dim.14.n_attn
  2.7 1.3 broadcast_in_dim.15.n_mlp
  4.0 4.2 fusion
  8.2 2.1 pad_maximum_fusion
  10.3 585.2 %decoder_layer.1 = (bf16[4608,5120]{1,0:T(8,128)(2,1)}, bf16[2304,128]{1,0:T(8,128)(2,1)}, bf16[2304,128]{1,0:T(8,128)(2,1)}) custom-call(bf16[2304,5120]{1,0:T(8,128)(2,1)} %bitcast.10, f32[2304,128]{1,0:T(8,128)} %get-tuple-element.15.cos_h, f32[2304,128]{1,0:T(8,128)} %get-tuple-element.16.sin_h, s32[3]{0:T(128)} %lens.1, ...), custom_call_target="tpu_custom_call" | custom-call | tf_op jit(solution)/shard_map/decoder_layer/pallas_call | solution.py:418
  595.5 0.0 copy-start.1
  595.5 19.6 %slice.3 = bf16[2304,5120]{1,0:T(8,128)(2,1)} slice(bf16[4608,5120]{1,0:T(8,128)(2,1)} %get-tuple-element.6), slice={[2304:4608], [0:5120]} | slice | bytes 47185920 | tf_op jit(solution)/shard_map/slice | solution.py:445
  615.1 0.0 copy-start
  615.1 0.0 copy-done.1
  615.1 0.8 copy.21
  616.0 0.5 copy-done
  616.4 0.8 copy.22
  (2 shorter events, 0.0 us)
Async XLA Ops:
  595.5 19.6 %copy-start.1 = (bf16[2304,128]{1,0:T(8,128)(2,1)S(1)}, bf16[2304,128]{1,0:T(8,128)(2,1)}, u32[]{:S(2)}) copy-start(bf16[2304,128]{1,0:T(8,128)(2,1)} %get-tuple-element.7) | copy-start | bytes 1769476
  615.1 1.3 copy-start
